TPU v7x, 8 devices: a whole 2x2x1 slice. The times are simulated.
8 devices in a mesh: row: 4 (over z, y, x), col: 2 (over core).
Axes of the slice: x: 2, y: 2, z: 1, core: 2. Of those that a mesh axis runs over, the one named last changes fastest.
Arguments:
- v_mat: float32 [8192, 8192], P('row', 'col')
- t_fac: float32 [128, 64, 64], P('col')
- z_vec: float32 [8192, 2048], P(None, ('col', 'row'))
Outputs:
- output: float32 [8192, 2048], P('row', 'col')
All inputs are finite; a program needn't handle non-finite values.
Results may differ from a plain program's by a relative error of at most 0.001.
Values sent between devices are 32-bit elements.
A program may use at most 1 GiB of HBM per device.

v0:
```python
import jax
import jax.numpy as jnp
from jax import lax
from jax.sharding import PartitionSpec as P

FULL_PREC = lax.Precision.HIGHEST


def solution(mesh):
    col_shards = mesh.shape['col']

    def local_body(v_loc, t_loc, z_loc):
        panel_width = t_loc.shape[1]
        local_panels = t_loc.shape[0]
        num_panels = local_panels * col_shards
        my_col = lax.axis_index('col')
        t_all = lax.all_gather(t_loc, 'col', axis=0, tiled=True)
        x_loc = lax.all_to_all(z_loc, 'row', 0, 1, tiled=True)

        def panel_step(step_idx, x_cur):
            panel_idx = num_panels - 1 - step_idx
            owner_col = panel_idx % col_shards
            loc_slot = panel_idx // col_shards
            v_blk = lax.dynamic_slice_in_dim(v_loc, loc_slot * panel_width, panel_width, axis=1)
            v_pan = lax.psum(jnp.where(my_col == owner_col, v_blk, 0.0), 'col')
            t_pan = lax.dynamic_index_in_dim(t_all, owner_col * local_panels + loc_slot, axis=0, keepdims=False)
            w_part = jnp.einsum('nb,nk->bk', v_pan, x_cur, preferred_element_type=jnp.float32, precision=FULL_PREC)
            w_full = lax.psum(w_part, 'row')
            y_blk = jnp.dot(t_pan, w_full, preferred_element_type=jnp.float32, precision=FULL_PREC)
            return x_cur - jnp.dot(v_pan, y_blk, preferred_element_type=jnp.float32, precision=FULL_PREC)

        return lax.fori_loop(0, num_panels, panel_step, x_loc)

    return jax.shard_map(local_body, mesh=mesh,
                         in_specs=(P('row', 'col'), P('col', None, None), P(None, ('col', 'row'))),
                         out_specs=P('row', 'col'), check_vma=False)
```

profile of v0, /device:TPU:0, one launch (start us, length us, event | category | flops | bytes accessed | tf_op | source)
XLA Modules:
  0.0 9250.4 jit_solution(17995155768557423788)
XLA Ops:
  12.9 93.3 %all-to-all-done = f32[4,2048,256]{2,1,0:T(8,128)} async-done(((f32[4,2048,256]{2,1,0:T(8,128)}), f32[4,2048,256]{2,1,0:T(8,128)}, u32[]{:S(2)}, u32[]{:S(2)}) %all-to-all-start) | async-done | bytes 8388640 | tf_op jit(solution)/shard_map/all_to_all | solution.py:18
  124.1 9119.4 %while.15 = (s32[]{:T(128)}, f32[2048,1024]{1,0:T(8,128)}, s32[]{:T(128)}, f32[2048,4096]{1,0:T(8,128)}, f32[128,64,64]{2,1,0:T(8,128)}, /*index=5*/s32[]{:T(128...) while((s32[]{:T(128)}, f32[2048,1024]{1,0:T(8,128)}, ...), condition=%wide.region_3.4_spmd, body=%wide.region_0.3_spmd.sunk | while | flops 3273981952 | bytes 36209192 | solution.py:32
  292.8 32.9 all-reduce.5.cloned.1.call-done
  577.5 32.9 all-reduce.5.cloned.1.call-done
  862.2 32.9 all-reduce.5.cloned.1.call-done
  1146.8 32.9 all-reduce.5.cloned.1.call-done
  1646.3 32.9 all-reduce.5.cloned.1.call-done
  2074.1 32.9 all-reduce.5.cloned.1.call-done
  2145.2 32.9 all-reduce.5.cloned.1.call-done
  2359.1 32.9 all-reduce.5.cloned.1.call-done
  2857.3 32.9 all-reduce.5.cloned.1.call-done
  3070.9 32.9 all-reduce.5.cloned.1.call-done
  3498.4 32.9 all-reduce.5.cloned.1.call-done
  3712.0 32.9 all-reduce.5.cloned.1.call-done
  3854.5 32.9 all-reduce.5.cloned.1.call-done
  3997.3 32.9 all-reduce.5.cloned.1.call-done
  4140.1 32.9 all-reduce.5.cloned.1.call-done
  4425.3 32.9 all-reduce.5.cloned.1.call-done
  4639.3 32.9 all-reduce.5.cloned.1.call-done
  4995.0 32.9 all-reduce.5.cloned.1.call-done
  5208.3 32.9 all-reduce.5.cloned.1.call-done
  5706.5 32.9 all-reduce.5.cloned.1.call-done
  5849.3 32.9 all-reduce.5.cloned.1.call-done
  6348.5 32.9 all-reduce.5.cloned.1.call-done
  6491.0 32.9 all-reduce.5.cloned.1.call-done
  6919.1 32.9 all-reduce.5.cloned.1.call-done
  7204.4 32.9 all-reduce.5.cloned.1.call-done
  7560.7 32.9 all-reduce.5.cloned.1.call-done
  7703.5 32.9 all-reduce.5.cloned.1.call-done
  7917.3 32.9 all-reduce.5.cloned.1.call-done
  8771.7 32.9 all-reduce.5.cloned.1.call-done
  9198.5 32.9 all-reduce.5.cloned.1.call-done
  (1512 shorter events, 8150.2 us)
Async XLA Ops:
  6.5 99.7 %all-to-all-start = ((f32[4,2048,256]{2,1,0:T(8,128)}), f32[4,2048,256]{2,1,0:T(8,128)}, u32[]{:S(2)}, u32[]{:S(2)}) async-start(f32[4,2048,256]{2,1,0:T(8,128)} %bitcast.25), calls=%async_computation | async-start | bytes 16777216 | tf_op jit(solution)/shard_map/all_to_all | solution.py:18
  12.2 111.9 %all-gather.2.cloned.1.call-start = ((), (), s32[]{:S(2)}) async-start(), calls=%async_computation.1 | async-start | bytes 6291456 | tf_op jit(solution)/shard_map/all_gather | solution.py:17
  126.8 56.8 all-reduce.5.cloned.1.call-start
  838.4 56.6 all-reduce.5.cloned.1.call-start
  1194.5 56.6 all-reduce.5.cloned.1.call-start
  1265.9 56.6 all-reduce.5.cloned.1.call-start
  1408.4 56.6 all-reduce.5.cloned.1.call-start
  1622.6 56.6 all-reduce.5.cloned.1.call-start
  1836.2 56.6 all-reduce.5.cloned.1.call-start
  2050.4 56.6 all-reduce.5.cloned.1.call-start
  2477.9 56.6 all-reduce.5.cloned.1.call-start
  2833.6 56.6 all-reduce.5.cloned.1.call-start
  3260.8 56.6 all-reduce.5.cloned.1.call-start
  3474.7 56.6 all-reduce.5.cloned.1.call-start
  3688.3 56.6 all-reduce.5.cloned.1.call-start
  3830.8 56.6 all-reduce.5.cloned.1.call-start
  3973.6 56.6 all-reduce.5.cloned.1.call-start
  4116.4 56.6 all-reduce.5.cloned.1.call-start
  4401.6 56.6 all-reduce.5.cloned.1.call-start
  4544.1 56.6 all-reduce.5.cloned.1.call-start
  4615.6 56.6 all-reduce.5.cloned.1.call-start
  4971.3 56.6 all-reduce.5.cloned.1.call-start
  5327.1 56.6 all-reduce.5.cloned.1.call-start
  5682.8 56.6 all-reduce.5.cloned.1.call-start
  5825.6 56.6 all-reduce.5.cloned.1.call-start
  6110.9 56.6 all-reduce.5.cloned.1.call-start
  6253.4 56.6 all-reduce.5.cloned.1.call-start
  6324.8 56.6 all-reduce.5.cloned.1.call-start
  6467.3 56.6 all-reduce.5.cloned.1.call-start
  6681.2 56.6 all-reduce.5.cloned.1.call-start
  6895.4 56.6 all-reduce.5.cloned.1.call-start
  8747.9 56.6 all-reduce.5.cloned.1.call-start
  (354 other events, 13254.5 us)
Sparse Core Ops, SparseCore 0:
  292.9 32.7 all-reduce.4
  577.6 32.7 all-reduce.4
  862.3 32.7 all-reduce.4
  1146.9 32.7 all-reduce.4
  1218.3 32.7 all-reduce.4
  1289.7 32.7 all-reduce.4
  1646.4 32.7 all-reduce.4
  1717.5 32.7 all-reduce.4
  2074.2 32.7 all-reduce.4
  2145.3 32.7 all-reduce.4
  2359.2 32.7 all-reduce.4
  2857.4 32.7 all-reduce.4
  3071.0 32.7 all-reduce.4
  3498.5 32.7 all-reduce.4
  3712.1 32.7 all-reduce.4
  3854.6 32.7 all-reduce.4
  3997.4 32.7 all-reduce.4
  4140.2 32.7 all-reduce.4
  4639.4 32.7 all-reduce.4
  4995.1 32.7 all-reduce.4
  5208.4 32.7 all-reduce.4
  5706.6 32.7 all-reduce.4
  5849.4 32.7 all-reduce.4
  6348.6 32.7 all-reduce.4
  6491.1 32.7 all-reduce.4
  6919.2 32.7 all-reduce.4
  7204.5 32.7 all-reduce.4
  7560.8 32.7 all-reduce.4
  7703.6 32.7 all-reduce.4
  7917.5 32.7 all-reduce.4
  8771.8 32.7 all-reduce.4
  9198.6 32.7 all-reduce.4
  (225 shorter events, 4871.1 us)
where the time goes:
time: 9260 us; the launch traced here: 9250 us
  waiting for transfers between devices  6070 us (66%)
  matrix products  2790 us (30%)
  other arithmetic  332 us (4%)
    psum x128, waiting for transfers between devices, panel_step(): w_full = lax.psum(w_part, 'row')  4210 us
    psum x128, waiting for transfers between devices, panel_step(): v_pan = lax.psum(jnp.where(my_col == owner_col, v_blk, 0.0), 'col')  1770 us
    dot_general x128, matrix products, panel_step(): jnp.dot(v_pan, y_blk, preferred_element_type=jnp.float32, precision=FULL_...  1390 us
    dot_general x128, matrix products, panel_step(): jnp.einsum('nb,nk->bk', v_pan, x_cur, preferred_element_type=jnp.float32,...  1230 us
    select_n x128, other arithmetic, panel_step(): v_pan = lax.psum(jnp.where(my_col == owner_col, v_blk, 0.0), 'col')  332 us
  transfers between devices with their start and end apart: 258, of which 257 were waited for; matrix products, arithmetic and copies ran while one was open for 0% of the time, Pallas kernels for 0%

commit v1 on v0

v1 whole, which is shorter than its diff:
```python
import functools

import jax
import jax.numpy as jnp
from jax import lax
from jax.experimental import pallas as pl
from jax.experimental.pallas import tpu as pltpu
from jax.sharding import PartitionSpec as P

MESH = pl.DeviceIdType.MESH
HIGHEST = lax.Precision.HIGHEST
F32, BF16 = jnp.float32, jnp.bfloat16

STEPS = 32
TILE = 256
LOC_ROWS = 2048
OWN_AHEAD = 6
FWD_AHEAD = 3
DIAG_AHEAD = 1

NN = (((1,), (0,)), ((), ()))
NT = (((1,), (1,)), ((), ()))
TN = (((0,), (0,)), ((), ()))


def dot32(a, b, dims=NN):
    return lax.dot_general(a, b, dims, precision=HIGHEST, preferred_element_type=F32)


def dotb(a, b, dims=NN):
    return lax.dot_general(a, b, dims, preferred_element_type=F32)


def split3(x):
    hi = x.astype(BF16)
    rest = x - hi.astype(F32)
    mid = rest.astype(BF16)
    low = (rest - mid.astype(F32)).astype(BF16)
    return hi, mid, low


def six(a, b, dims):
    ah, am, al = a
    bh, bm, bl = b
    return (dotb(ah, bh, dims) + dotb(ah, bm, dims) + dotb(am, bh, dims)
            + dotb(am, bm, dims) + dotb(ah, bl, dims) + dotb(al, bh, dims))


X_DIR, Y_DIR, Y_FWD, X_FWD, S_OWN, S_X, S_Y, S_DA, S_DB = range(9)


def kernel(v_ref, t_ref, z_ref, out_ref, g_ref,
           xt, vbuf, vs, stage, t_own, t_sib, dmat, wt, gm, yt,
           send_sem, recv_sem, load_sem, aux_sem, fin_send, fin_recv,
           *, comm=True, compute=True):
    r = lax.axis_index("row")
    c = lax.axis_index("col")
    rx = r + 1 - 2 * lax.rem(r, 2)
    ry = lax.rem(r + 2, 4)
    rd = 3 - r
    dev_x, dev_y, dev_d, dev_s = (rx, c), (ry, c), (rd, c), (r, 1 - c)
    peer_row = (r, rx, ry, rd)

    barrier = pltpu.get_barrier_semaphore()
    for dev in (dev_x, dev_y, dev_d, dev_s):
        pl.semaphore_signal(barrier, inc=1, device_id=dev, device_id_type=MESH)
    pl.semaphore_wait(barrier, 4)

    def win(n, part=None):
        m = STEPS - 1 - n
        lo, rows = 64 * m, 64 * (n + 1)
        if part == 0:
            rows = rows // 2
        elif part == 1:
            lo, rows = lo + rows // 2, rows // 2
        return pl.ds(lo, rows), pl.ds(128 * m, 128)

    def mk(cls, n):
        part = {Y_FWD: 0, S_DA: 0, X_FWD: 1, S_DB: 1}.get(cls)
        a, b = win(n, part)
        own = v_ref.at[a, b]
        if cls == X_DIR:
            src, dst, dev = own, g_ref.at[1, 0, a, b], dev_x
        elif cls == Y_DIR:
            src, dst, dev = own, g_ref.at[2, 0, a, b], dev_y
        elif cls == Y_FWD:
            src, dst, dev = g_ref.at[1, 0, a, b], g_ref.at[3, 0, a, b], dev_y
        elif cls == X_FWD:
            src, dst, dev = g_ref.at[2, 0, a, b], g_ref.at[3, 0, a, b], dev_x
        elif cls == S_OWN:
            src, dst, dev = own, g_ref.at[0, 1, a, b], dev_s
        elif cls == S_X:
            src, dst, dev = g_ref.at[1, 0, a, b], g_ref.at[1, 1, a, b], dev_s
        elif cls == S_Y:
            src, dst, dev = g_ref.at[2, 0, a, b], g_ref.at[2, 1, a, b], dev_s
        else:
            src, dst, dev = g_ref.at[3, 0, a, b], g_ref.at[3, 1, a, b], dev_s
        return pltpu.make_async_remote_copy(
            src_ref=src, dst_ref=dst, send_sem=send_sem.at[cls, n],
            recv_sem=recv_sem.at[cls, n], device_id=dev, device_id_type=MESH)

    def own_send(n):
        for cls in (X_DIR, Y_DIR, S_OWN):
            mk(cls, n).start()

    def forward(n):
        mk(X_DIR, n).wait_recv()
        mk(Y_FWD, n).start()
        mk(S_X, n).start()
        mk(Y_DIR, n).wait_recv()
        mk(X_FWD, n).start()
        mk(S_Y, n).start()

    def share_diag(n):
        mk(Y_FWD, n).wait_recv()
        mk(S_DA, n).start()
        mk(X_FWD, n).wait_recv()
        mk(S_DB, n).start()

    def sib_wait(n):
        for cls in (S_OWN, S_X, S_Y, S_DA, S_DB):
            mk(cls, n).wait_recv()

    def vloads(n):
        a, b = win(n)
        cps = []
        for k in range(4):
            for cc in range(2):
                src = v_ref.at[a, b] if (k == 0 and cc == 0) else g_ref.at[k, cc, a, b]
                cps.append(pltpu.make_async_copy(
                    src, vbuf.at[k, a, pl.ds(128 * cc, 128)], load_sem.at[2 * k + cc]))
        return cps

    fwd_at = {n: [] for n in range(-1, STEPS)}
    diag_at = {n: [] for n in range(-1, STEPS)}
    for n in range(STEPS):
        fwd_at[max(n - FWD_AHEAD, -1) if n < STEPS - 1 else n - 2].append(n)
        diag_at[max(n - DIAG_AHEAD, -1) if n < STEPS - 1 else n].append(n)

    t_local = pltpu.make_async_copy(t_ref, t_own, aux_sem.at[0])
    t_local.start()
    t_remote = pltpu.make_async_remote_copy(
        src_ref=t_ref, dst_ref=t_sib, send_sem=aux_sem.at[1], recv_sem=aux_sem.at[2],
        device_id=dev_s, device_id_type=MESH)
    t_remote.start()
    zl = [pltpu.make_async_copy(
        z_ref.at[pl.ds(pl.multiple_of(peer_row[k] * LOC_ROWS, LOC_ROWS), LOC_ROWS), :],
        stage.at[k], aux_sem.at[3 + k]) for k in range(4)]
    for cp in zl:
        cp.start()
    if comm:
        for n in range(OWN_AHEAD):
            own_send(n)

    vbuf[...] = jnp.zeros_like(vbuf)
    dmat[...] = jnp.zeros_like(dmat)
    for cp in zl:
        cp.wait()

    @pl.loop(0, 32)
    def _(t):
        k, i4 = lax.rem(t, 4), t // 4
        xt[t] = stage[k, pl.ds(pl.multiple_of(i4 * TILE, TILE), TILE), :].T

    t_local.wait()
    t_remote.wait()
    if comm:
        for n in fwd_at[-1]:
            forward(n)
        for n in diag_at[-1]:
            share_diag(n)

    def order(dim):
        pos = lax.broadcasted_iota(jnp.int32, (TILE, TILE), dim) // 64
        core = pos // 2
        return 2 * (pos - 2 * core) + core + c - 2 * core * c

    def block(n):
        m = STEPS - 1 - n
        first = 4 * (m // 4)
        for i in range(2):
            dmat[64 * i:64 * i + 64, 64 * i:64 * i + 64] = t_own[2 * m + i]
            dmat[128 + 64 * i:192 + 64 * i, 128 + 64 * i:192 + 64 * i] = t_sib[2 * m + i]
        wt[...] = jnp.zeros_like(wt)
        gm[...] = jnp.zeros_like(gm)

        @pl.loop(first, 32)
        def _(t):
            k, i4 = lax.rem(t, 4), t // 4
            v = split3(vbuf[k, pl.ds(pl.multiple_of(i4 * TILE, TILE), TILE), :])
            for i in range(3):
                vs[i, t] = v[i]
            x = split3(xt[t])
            wt[...] += six(x, v, NN)
            gm[0] += dotb(v[0], v[0], TN) + dotb(v[1], v[1], TN)
            gm[1] += dotb(v[0], v[1], TN) + dotb(v[0], v[2], TN)

        cross = gm[1]
        gram = gm[0] + cross + cross.T
        upper = jnp.where(order(0) < order(1), gram, 0.0)
        diag = dmat[...]
        nil = dot32(diag, upper)
        sq = dot32(nil, nil)
        eye = (lax.broadcasted_iota(jnp.int32, (TILE, TILE), 0)
               == lax.broadcasted_iota(jnp.int32, (TILE, TILE), 1)).astype(F32)
        big = dot32(dot32(eye - nil, eye + sq), diag)
        y = split3(dot32(wt[...], big, NT))
        for i in range(3):
            yt[i] = y[i]

        @pl.loop(first, 32)
        def _(t):
            xt[t] -= six((yt[0], yt[1], yt[2]), (vs[0, t], vs[1, t], vs[2, t]), NT)

    @pl.loop(0, STEPS)
    def _(n):
        for k in range(STEPS):
            @pl.when(n == k)
            def _(k=k):
                if comm:
                    if k + OWN_AHEAD < STEPS:
                        own_send(k + OWN_AHEAD)
                    for j in fwd_at[k]:
                        forward(j)
                    for j in diag_at[k]:
                        share_diag(j)
                    sib_wait(k)
                loads = vloads(k)
                for cp in loads:
                    cp.start()
                for cp in loads:
                    cp.wait()
        if compute:
            block(n)

    finals = {}
    for k in (3, 1, 2, 0):
        @pl.loop(0, 8)
        def _(i4, k=k):
            stage[k, pl.ds(pl.multiple_of(i4 * TILE, TILE), TILE), :] = xt[4 * i4 + k].T
        cols = out_ref.at[:, pl.ds(pl.multiple_of(r * TILE, TILE), TILE)]
        if k:
            finals[k] = pltpu.make_async_remote_copy(
                src_ref=stage.at[k], dst_ref=cols, send_sem=fin_send.at[k],
                recv_sem=fin_recv.at[k], device_id=(peer_row[k], c), device_id_type=MESH)
        else:
            finals[k] = pltpu.make_async_copy(stage.at[0], cols, fin_send.at[0])
        finals[k].start()
    if comm:
        for n in range(STEPS):
            for cls in range(9):
                mk(cls, n).wait_send()
    for k in range(4):
        finals[k].wait()


def solution(mesh, comm=True, compute=True):
    def local_body(v_loc, t_loc, z_loc):
        any_spec = pl.BlockSpec(memory_space=pl.ANY)
        out, _ = pl.pallas_call(
            functools.partial(kernel, comm=comm, compute=compute),
            out_shape=(jax.ShapeDtypeStruct((LOC_ROWS, 4 * TILE), F32),
                       jax.ShapeDtypeStruct((4, 2, LOC_ROWS, 4096), F32)),
            in_specs=[any_spec] * 3,
            out_specs=(any_spec, any_spec),
            scratch_shapes=[
                pltpu.VMEM((32, TILE, TILE), F32),
                pltpu.VMEM((4, LOC_ROWS, TILE), F32),
                pltpu.VMEM((3, 32, TILE, TILE), BF16),
                pltpu.VMEM((4, LOC_ROWS, TILE), F32),
                pltpu.VMEM((64, 64, 64), F32),
                pltpu.VMEM((64, 64, 64), F32),
                pltpu.VMEM((TILE, TILE), F32),
                pltpu.VMEM((TILE, TILE), F32),
                pltpu.VMEM((2, TILE, TILE), F32),
                pltpu.VMEM((3, TILE, TILE), BF16),
                pltpu.SemaphoreType.DMA((9, STEPS)),
                pltpu.SemaphoreType.DMA((9, STEPS)),
                pltpu.SemaphoreType.DMA((8,)),
                pltpu.SemaphoreType.DMA((7,)),
                pltpu.SemaphoreType.DMA((4,)),
                pltpu.SemaphoreType.DMA((4,)),
            ],
            compiler_params=pltpu.CompilerParams(
                collective_id=0, has_side_effects=True, vmem_limit_bytes=60 * 2**20),
            name="apply_panels",
        )(v_loc, t_loc, z_loc)
        return out

    return jax.shard_map(local_body, mesh=mesh,
                         in_specs=(P('row', 'col'), P('col', None, None), P(None, ('col', 'row'))),
                         out_specs=P('row', 'col'), check_vma=False)
```

time: 9260 us -> 858 us (0.09)
  waiting for transfers between devices: 6070 us -> 0 us
  matrix products: 2790 us -> 0 us
  Pallas kernels: 0 us -> 849 us
  other arithmetic: 332 us -> 0 us
    psum x256 -> x0, waiting for transfers between devices: 5980 us -> none  [the longest x128 4210 us: panel_step(): w_full = lax.psum(w_part, 'row')]
    dot_general x384 -> x0, matrix products: 2790 us -> none  [the longest x128 1390 us: panel_step(): jnp.dot(v_pan, y_blk, preferred_element_type=jnp.float32, precision=FULL_...]
    pallas_call x0 -> x1, Pallas kernels: none -> 849 us  [local_body(): pl.pallas_call(functools.partial(kernel, comm=comm, compute=compute), out...]
    select_n x128 -> x0, other arithmetic: 332 us -> none  [panel_step(): v_pan = lax.psum(jnp.where(my_col == owner_col, v_blk, 0.0), 'col')]
    all_to_all x1 -> x0, waiting for transfers between devices: 93.3 us -> none  [local_body(): x_loc = lax.all_to_all(z_loc, 'row', 0, 1, tiled=True)]
  transfers between devices with their start and end apart: 258 -> 0, of which waited for: 257 -> 0; matrix products, arithmetic and copies ran while one was open for 0% -> 0% of each run, Pallas kernels for 0% -> 0%
where the time goes in v1:
time: 858 us
  Pallas kernels  849 us (99%)
    pallas_call x1, Pallas kernels, local_body(): pl.pallas_call(functools.partial(kernel, comm=comm, compute=compute), out...  849 us

profile of v1, /device:TPU:0, one launch (start us, length us, event | category | flops | bytes accessed | tf_op | source)
XLA Modules:
  0.0 857.6 jit_solution(6696184191338328609)
XLA Ops:
  0.0 849.2 %apply_panels.1 = (f32[2048,1024]{1,0:T(8,128)}, f32[4,2,2048,4096]{3,2,1,0:T(8,128)}) custom-call(f32[2048,4096]{1,0:T(8,128)} %v_ref.1, f32[64,64,64]{2,1,0:T(8,128)} %t_ref.1, f32[8192,256]{1,0:T(8,128)} %z_ref.1), custom_call_target="tpu_custom_call" | custom-call | tf_op jit(solution)/shard_map/apply_panels/pallas_call | solution.py:260
  849.2 8.4 copy.5

commit v2 on v1

--- a/solution.py
+++ b/solution.py
@@ -14,9 +14,22 @@
 STEPS = 32
 TILE = 256
 LOC_ROWS = 2048
-OWN_AHEAD = 6
-FWD_AHEAD = 3
-DIAG_AHEAD = 1
+
+
+def ahead(n, early, late):
+    return early if n < 14 else max(late, early - (n - 14))
+
+
+def plan(early, late):
+    at = {k: [] for k in range(-1, STEPS)}
+    for n in range(STEPS):
+        at[max(n - ahead(n, early, late), -1)].append(n)
+    return at
+
+
+OWN_AT = plan(8, 4)
+FWD_AT = plan(4, 3)
+DIAG_AT = plan(2, 1)
 
 NN = (((1,), (0,)), ((), ()))
 NT = (((1,), (1,)), ((), ()))
@@ -40,10 +53,10 @@
 
 
 def six(a, b, dims):
-    ah, am, al = a
-    bh, bm, bl = b
-    return (dotb(ah, bh, dims) + dotb(ah, bm, dims) + dotb(am, bh, dims)
-            + dotb(am, bm, dims) + dotb(ah, bl, dims) + dotb(al, bh, dims))
+    (ldim,), (rdim,) = dims[0]
+    lhs = [x[i] for x in a for i in (0, 0, 1, 1, 0, 2)]
+    rhs = [x[i] for x in b for i in (0, 1, 0, 1, 2, 0)]
+    return dotb(jnp.concatenate(lhs, axis=ldim), jnp.concatenate(rhs, axis=rdim), dims)
 
 
 X_DIR, Y_DIR, Y_FWD, X_FWD, S_OWN, S_X, S_Y, S_DA, S_DB = range(9)
@@ -131,12 +144,6 @@
                     src, vbuf.at[k, a, pl.ds(128 * cc, 128)], load_sem.at[2 * k + cc]))
         return cps
 
-    fwd_at = {n: [] for n in range(-1, STEPS)}
-    diag_at = {n: [] for n in range(-1, STEPS)}
-    for n in range(STEPS):
-        fwd_at[max(n - FWD_AHEAD, -1) if n < STEPS - 1 else n - 2].append(n)
-        diag_at[max(n - DIAG_AHEAD, -1) if n < STEPS - 1 else n].append(n)
-
     t_local = pltpu.make_async_copy(t_ref, t_own, aux_sem.at[0])
     t_local.start()
     t_remote = pltpu.make_async_remote_copy(
@@ -149,7 +156,7 @@
     for cp in zl:
         cp.start()
     if comm:
-        for n in range(OWN_AHEAD):
+        for n in OWN_AT[-1]:
             own_send(n)
 
     vbuf[...] = jnp.zeros_like(vbuf)
@@ -165,79 +172,124 @@
     t_local.wait()
     t_remote.wait()
     if comm:
-        for n in fwd_at[-1]:
+        for n in FWD_AT[-1]:
             forward(n)
-        for n in diag_at[-1]:
+        for n in DIAG_AT[-1]:
             share_diag(n)
+        sib_wait(0)
+    for cp in vloads(0):
+        cp.start()
 
     def order(dim):
         pos = lax.broadcasted_iota(jnp.int32, (TILE, TILE), dim) // 64
         core = pos // 2
         return 2 * (pos - 2 * core) + core + c - 2 * core * c
 
-    def block(n):
+    def block(n, hook):
         m = STEPS - 1 - n
-        first = 4 * (m // 4)
         for i in range(2):
             dmat[64 * i:64 * i + 64, 64 * i:64 * i + 64] = t_own[2 * m + i]
             dmat[128 + 64 * i:192 + 64 * i, 128 + 64 * i:192 + 64 * i] = t_sib[2 * m + i]
         wt[...] = jnp.zeros_like(wt)
         gm[...] = jnp.zeros_like(gm)
 
-        @pl.loop(first, 32)
-        def _(t):
-            k, i4 = lax.rem(t, 4), t // 4
-            v = split3(vbuf[k, pl.ds(pl.multiple_of(i4 * TILE, TILE), TILE), :])
-            for i in range(3):
-                vs[i, t] = v[i]
-            x = split3(xt[t])
-            wt[...] += six(x, v, NN)
-            gm[0] += dotb(v[0], v[0], TN) + dotb(v[1], v[1], TN)
-            gm[1] += dotb(v[0], v[1], TN) + dotb(v[0], v[2], TN)
-
+        @pl.loop(m // 4, 8)
+        def _(i4):
+            rows = pl.ds(pl.multiple_of(i4 * TILE, TILE), TILE)
+            vt, xl = [], []
+            for k in range(4):
+                v = split3(vbuf[k, rows, :])
+                for i in range(3):
+                    vs[i, 4 * i4 + k] = v[i]
+                vt.append(v)
+                xl.append(split3(xt[4 * i4 + k]))
+            wt[...] += six(xl, vt, NN)
+            high = [v[i] for v in vt for i in (0, 1)]
+            high = jnp.concatenate(high, axis=0)
+            gm[0] += dotb(high, high, TN)
+            left = jnp.concatenate([v[0] for v in vt for i in (1, 2)], axis=0)
+            right = jnp.concatenate([v[i] for v in vt for i in (1, 2)], axis=0)
+            gm[1] += dotb(left, right, TN)
+
+        hook()
         cross = gm[1]
         gram = gm[0] + cross + cross.T
         upper = jnp.where(order(0) < order(1), gram, 0.0)
         diag = dmat[...]
         nil = dot32(diag, upper)
+        p0 = dot32(wt[...], diag, NT)
+        p1 = dot32(p0, nil, NT)
         sq = dot32(nil, nil)
-        eye = (lax.broadcasted_iota(jnp.int32, (TILE, TILE), 0)
-               == lax.broadcasted_iota(jnp.int32, (TILE, TILE), 1)).astype(F32)
-        big = dot32(dot32(eye - nil, eye + sq), diag)
-        y = split3(dot32(wt[...], big, NT))
+        p23 = dot32(jnp.concatenate([p0, p1], axis=0), sq, NT)
+        y = split3((p0 - p1) + (p23[:TILE] - p23[TILE:]))
         for i in range(3):
             yt[i] = y[i]
 
-        @pl.loop(first, 32)
-        def _(t):
-            xt[t] -= six((yt[0], yt[1], yt[2]), (vs[0, t], vs[1, t], vs[2, t]), NT)
+        @pl.loop(jnp.where(n == STEPS - 1, 8, m // 4), 8)
+        def _(i4):
+            for k in range(4):
+                t = 4 * i4 + k
+                xt[t] -= six([(yt[0], yt[1], yt[2])], [(vs[0, t], vs[1, t], vs[2, t])], NT)
+
+    def next_loads(n):
+        if comm:
+            sib_wait(n)
+        for cp in vloads(n):
+            cp.start()
+
+    def each(n, body):
+        for g in range(0, STEPS, 8):
+            @pl.when(n // 8 == g // 8)
+            def _(g=g):
+                for k in range(g, g + 8):
+                    pl.when(n == k)(functools.partial(body, k))
+
+    def top(k):
+        if comm:
+            for n in OWN_AT[k]:
+                own_send(n)
+            for n in FWD_AT[k]:
+                if n < STEPS - 1:
+                    forward(n)
+            for n in DIAG_AT[k]:
+                if n < STEPS - 1:
+                    share_diag(n)
+        for cp in vloads(k):
+            cp.wait()
+
+    def middle(k):
+        if comm and STEPS - 1 in FWD_AT[k]:
+            forward(STEPS - 1)
+        if k + 1 < STEPS - 2:
+            next_loads(k + 1)
 
     @pl.loop(0, STEPS)
     def _(n):
-        for k in range(STEPS):
-            @pl.when(n == k)
-            def _(k=k):
-                if comm:
-                    if k + OWN_AHEAD < STEPS:
-                        own_send(k + OWN_AHEAD)
-                    for j in fwd_at[k]:
-                        forward(j)
-                    for j in diag_at[k]:
-                        share_diag(j)
-                    sib_wait(k)
-                loads = vloads(k)
-                for cp in loads:
-                    cp.start()
-                for cp in loads:
-                    cp.wait()
+        each(n, top)
         if compute:
-            block(n)
+            block(n, lambda: each(n, middle))
+        else:
+            each(n, middle)
+
+        @pl.when(n == STEPS - 3)
+        def _():
+            next_loads(STEPS - 2)
+
+        @pl.when(n == STEPS - 2)
+        def _():
+            if comm:
+                share_diag(STEPS - 1)
+            next_loads(STEPS - 1)
 
     finals = {}
     for k in (3, 1, 2, 0):
         @pl.loop(0, 8)
         def _(i4, k=k):
-            stage[k, pl.ds(pl.multiple_of(i4 * TILE, TILE), TILE), :] = xt[4 * i4 + k].T
+            t = 4 * i4 + k
+            done = xt[t]
+            if compute:
+                done -= six([(yt[0], yt[1], yt[2])], [(vs[0, t], vs[1, t], vs[2, t])], NT)
+            stage[k, pl.ds(pl.multiple_of(i4 * TILE, TILE), TILE), :] = done.T
         cols = out_ref.at[:, pl.ds(pl.multiple_of(r * TILE, TILE), TILE)]
         if k:
             finals[k] = pltpu.make_async_remote_copy(

time: 858 us -> 733 us (0.85)
  Pallas kernels: 849 us -> 725 us
    pallas_call x1, Pallas kernels: 849 us -> 725 us  [local_body(): pl.pallas_call(functools.partial(kernel, comm=comm, compute=compute), out...]
where the time goes in v2:
time: 733 us
  Pallas kernels  725 us (99%)
  local copies, waits for them, and re-layouts  8.44 us (1%)
    pallas_call x1, Pallas kernels, local_body(): pl.pallas_call(functools.partial(kernel, comm=comm, compute=compute), out...  725 us

profile of v2, /device:TPU:0, one launch (start us, length us, event | category | flops | bytes accessed | tf_op | source)
XLA Modules:
  0.0 733.0 jit_solution(13036146918981067088)
XLA Ops:
  0.0 724.5 %apply_panels.1 = (f32[2048,1024]{1,0:T(8,128)}, f32[4,2,2048,4096]{3,2,1,0:T(8,128)}) custom-call(f32[2048,4096]{1,0:T(8,128)} %v_ref.1, f32[64,64,64]{2,1,0:T(8,128)} %t_ref.1, f32[8192,256]{1,0:T(8,128)} %z_ref.1), custom_call_target="tpu_custom_call" | custom-call | tf_op jit(solution)/shard_map/apply_panels/pallas_call | solution.py:312
  724.5 8.4 %copy.5 = f32[2048,1024]{1,0:T(8,128)} copy(f32[2048,1024]{1,0:T(8,128)} %get-tuple-element.6) | data formatting | bytes 16777216

commit v3 on v2

--- a/solution.py
+++ b/solution.py
@@ -27,7 +27,7 @@
     return at
 
 
-OWN_AT = plan(8, 4)
+OWN_AT = plan(6, 4)
 FWD_AT = plan(4, 3)
 DIAG_AT = plan(2, 1)
 

time: 733 us -> 731 us (level)
  no operation moved by 1% of the time
where the time goes in v3:
time: 731 us; the launch traced here: 730 us
  Pallas kernels  722 us (99%)
  local copies, waits for them, and re-layouts  8.44 us (1%)
    pallas_call x1, Pallas kernels, local_body(): pl.pallas_call(functools.partial(kernel, comm=comm, compute=compute), out...  722 us

profile of v3, /device:TPU:0, one launch (start us, length us, event | category | flops | bytes accessed | tf_op | source)
XLA Modules:
  0.0 730.4 jit_solution(5211429197346062823)
XLA Ops:
  0.0 722.0 %apply_panels.1 = (f32[2048,1024]{1,0:T(8,128)}, f32[4,2,2048,4096]{3,2,1,0:T(8,128)}) custom-call(f32[2048,4096]{1,0:T(8,128)} %v_ref.1, f32[64,64,64]{2,1,0:T(8,128)} %t_ref.1, f32[8192,256]{1,0:T(8,128)} %z_ref.1), custom_call_target="tpu_custom_call" | custom-call | tf_op jit(solution)/shard_map/apply_panels/pallas_call | solution.py:312
  722.0 8.4 %copy.5 = f32[2048,1024]{1,0:T(8,128)} copy(f32[2048,1024]{1,0:T(8,128)} %get-tuple-element.6) | data formatting | bytes 16777216
